TPU v7x, 256 devices: a whole 4x4x8 slice. The times are simulated.
256 devices in a mesh: row: 8 (over y, core), col: 32 (over z, x).
Axes of the slice: x: 4, y: 4, z: 8, core: 2. Of those that a mesh axis runs over, the one named last changes fastest.
Arguments:
- rhs: bfloat16 [6144, 6144], P('row', 'col'), may hold values from -6 to 6
- basis_left: bfloat16 [6144, 6144], P('col', 'row'), may hold values from -1 to 1, as said below
- basis_right: bfloat16 [6144, 6144], P('row', 'col'), may hold values from -1 to 1, as said below
- eig_left: float32 [6144], P('row'), may hold values from 0.1 to 4
- eig_right: float32 [6144], P('col'), may hold values from 0.1 to 4
Outputs:
- solution: bfloat16 [6144, 6144], P('col', 'row')
Inputs may be any that keep to these rules, and one draw needn't show every extreme that they name: `basis_left`: an orthogonal matrix drawn uniformly, rounded to bfloat16. `basis_right`: an orthogonal matrix drawn uniformly, rounded to bfloat16.
All inputs are finite; a program needn't handle non-finite values.
Results may differ from a plain program's by a relative error of at most 0.0085.
Values may be sent and summed in bfloat16 or wider, within the bound.
A program may use at most 64 MiB of HBM per device.

v0:
```python
import jax
import jax.numpy as jnp
from jax import lax
from jax.sharding import PartitionSpec as P


def laid_out(parts, dim):
    parts = jnp.moveaxis(parts, 0, dim)
    lengths = parts.shape
    return parts.reshape(*lengths[:dim], lengths[dim] * lengths[dim + 1], *lengths[dim + 2 :])


def sent_to_all(shard, axis):
    copies = jnp.broadcast_to(shard, (lax.axis_size(axis), *shard.shape))
    return lax.all_to_all(copies, axis, split_axis=0, concat_axis=0, tiled=True)


def gathered_copies(shard, axis, dim):
    return laid_out(sent_to_all(shard, axis), dim)


def in_blocks(shard, dim, peers):
    lengths = shard.shape
    parts = shard.reshape(*lengths[:dim], peers, lengths[dim] // peers, *lengths[dim + 1 :])
    return jnp.moveaxis(parts, dim, 0)


def sent_and_summed(shard, axis, dim):
    peers = lax.axis_size(axis)
    parts = lax.all_to_all(in_blocks(shard, dim, peers), axis, 0, 0, tiled=True)
    return jnp.sum(parts.astype(jnp.float32), axis=0)


def body(rhs, basis_left, basis_right, eig_left, eig_right):
    c_strip = gathered_copies(rhs, "row", 0)
    chosen = c_strip
    first = lax.dot_general(
        lax.all_gather(basis_left, "col", axis=0, tiled=True),
        chosen,
        (((0,), (0,)), ((), ())),
        preferred_element_type=jnp.float32,
    )
    projected = first.astype(jnp.bfloat16)
    right_strip = lax.all_gather(basis_right, "row", axis=0, tiled=True)
    chosen = right_strip
    second = jnp.dot(
        lax.all_gather(projected, "col", axis=1, tiled=True),
        chosen,
        preferred_element_type=jnp.float32,
    )
    scaled = (second / (eig_left[:, None] + eig_right[None, :])).astype(jnp.bfloat16)
    scaled_strip = lax.all_gather(scaled, "col", axis=1, tiled=True)
    chosen = scaled_strip
    half_turned = sent_and_summed(
        lax.dot_general(
            chosen, basis_left, (((0,), (1,)), ((), ())), preferred_element_type=jnp.float32
        ).astype(jnp.bfloat16),
        "row",
        0,
    ).astype(jnp.bfloat16)
    half_strip = gathered_copies(half_turned, "row", 0)
    chosen = half_strip
    turned = jnp.dot(
        lax.all_gather(basis_right, "col", axis=1, tiled=True),
        chosen,
        preferred_element_type=jnp.float32,
    )
    return turned.T.astype(jnp.bfloat16)


def solution(mesh):
    in_specs = (P("row", "col"), P("col", "row"), P("row", "col"), P("row"), P("col"))
    out_specs = P("col", "row")
    return jax.shard_map(body, mesh=mesh, in_specs=in_specs, out_specs=out_specs, check_vma=False)
```

profile of v0, /device:TPU:1, one launch (start us, length us, event | category | flops | bytes accessed | tf_op | source)
XLA Modules:
  0.0 472.5 jit_solution(11340699577800707060)
XLA Ops:
  6.5 0.0 all-gather.6.cloned.1.call-start
  6.5 0.7 all-gather.6.cloned.1.call-update
  7.3 0.0 all-gather.10.cloned.1.call-start
  7.3 0.7 all-gather.10.cloned.1.call-update
  8.0 0.0 all-gather.8.cloned.1.call-start
  8.1 1.1 broadcast_in_dim.8
  9.2 34.7 %all_to_all.15 = bf16[8,768,192]{1,2,0:T(8,128)(2,1)S(1)} all-to-all(bf16[8,768,192]{1,2,0:T(8,128)(2,1)S(1)} %broadcast_in_dim.8), channel_id=1, replica_groups=mesh['row'=8,'col'=32] {'row'}, dimensions={0} | all-to-all | bytes 4718592 | tf_op jit(solution)/shard_map/all_to_all | solution.py:15
  43.9 0.3 copy.15
  44.2 71.9 %all-gather.6.cloned.1.call-done = bf16[6144,768]{1,0:T(8,128)(2,1)} async-done(((bf16[192,768]{1,0:T(8,128)(2,1)}), bf16[6144,768]{1,0:T(8,128)(2,1)}) %all-gather.6.cloned.1.call-update) | async-done | bytes 9437200 | tf_op jit(solution)/shard_map/all_gather | solution.py:38
  116.1 6.4 %convolution_convert_fusion.1 = bf16[768,192]{0,1:T(8,128)(2,1)} fusion(bf16[6144,192]{0,1:T(8,128)(2,1)S(1)} %bitcast.19, bf16[6144,768]{1,0:T(8,128)(2,1)} %all-gather.6.cloned.1.call-done), kind=kOutput, calls=%fused_computation.2 | convolution fusion | flops 1812086784 | bytes 12091392 | tf_op jit(solution)/shard_map/dot_general | solution.py:37
  122.5 0.0 all-gather.8.cloned.1.call-update
  122.5 0.0 copy-start
  122.5 0.0 all-gather.12.cloned.1.call-start
  122.6 21.8 %all-gather.10.cloned.1.call-done = bf16[6144,192]{0,1:T(8,128)(2,1)} async-done(((bf16[768,192]{0,1:T(8,128)(2,1)}), bf16[6144,192]{0,1:T(8,128)(2,1)}) %all-gather.10.cloned.1.call-update) | async-done | bytes 2359312 | tf_op jit(solution)/shard_map/all_gather | solution.py:44
  144.3 105.2 %all-gather.8.cloned.1.call-done = bf16[768,6144]{0,1:T(8,128)(2,1)} async-done(((bf16[768,192]{0,1:T(8,128)(2,1)}), bf16[768,6144]{0,1:T(8,128)(2,1)}) %all-gather.8.cloned.1.call-update) | async-done | bytes 9437200 | tf_op jit(solution)/shard_map/all_gather | solution.py:47
  249.5 0.0 copy-done.1
  249.5 0.0 copy-done.2
  249.5 7.1 %fusion = bf16[768,192]{0,1:T(8,128)(2,1)} fusion(bf16[6144,192]{0,1:T(8,128)(2,1)} %all-gather.10.cloned.1.call-done, bf16[768,6144]{0,1:T(8,128)(2,1)} %all-gather.8.cloned.1.call-done, f32[192]{0:T(256)S(1)} %copy-done.2, f32[768]{0:T(1024)S(1)} %copy-done.1), kind=kOutput, calls=%fused_computation.5 | convolution fusion | flops 1812381696 | bytes 12095232 | tf_op jit(solution)/shard_map/dot_general | solution.py:46
  256.6 0.0 all-gather.12.cloned.1.call-update
  256.6 0.0 all-gather.14.cloned.1.call-start
  256.7 0.5 all-gather.14.cloned.1.call-update
  257.2 99.8 %all-gather.12.cloned.1.call-done = bf16[768,6144]{0,1:T(8,128)(2,1)} async-done(((bf16[768,192]{0,1:T(8,128)(2,1)}), bf16[768,6144]{0,1:T(8,128)(2,1)}) %all-gather.12.cloned.1.call-update) | async-done | bytes 9437200 | tf_op jit(solution)/shard_map/all_gather | solution.py:52
  357.0 0.0 copy-done
  357.0 6.9 %convolution_convert_fusion = bf16[6144,192]{0,1:T(8,128)(2,1)S(1)} fusion(bf16[768,6144]{0,1:T(8,128)(2,1)} %all-gather.12.cloned.1.call-done, bf16[192,768]{1,0:T(8,128)(2,1)S(1)} %copy-done), kind=kOutput, calls=%fused_computation | convolution fusion | flops 1813118976 | bytes 12091392 | tf_op jit(solution)/shard_map/dot_general | solution.py:55
  363.9 0.2 copy.18
  364.0 34.5 %all_to_all.16 = bf16[8,768,192]{1,2,0:T(8,128)(2,1)S(1)} all-to-all(bf16[8,768,192]{1,2,0:T(8,128)(2,1)S(1)} %bitcast.17), channel_id=1, replica_groups=mesh['row'=8,'col'=32] {'row'}, dimensions={0} | all-to-all | bytes 4718592 | tf_op jit(solution)/shard_map/all_to_all | solution.py:30
  398.5 0.4 reduce_sum.12
  398.9 0.2 broadcast_in_dim.9
  399.1 32.5 %all_to_all.17 = bf16[8,768,192]{1,2,0:T(8,128)(2,1)S(1)} all-to-all(bf16[8,768,192]{1,2,0:T(8,128)(2,1)S(1)} %broadcast_in_dim.9), channel_id=1, replica_groups=mesh['row'=8,'col'=32] {'row'}, dimensions={0} | all-to-all | bytes 4718592 | tf_op jit(solution)/shard_map/all_to_all | solution.py:15
  431.6 0.3 copy.16
  431.9 27.7 %all-gather.14.cloned.1.call-done = bf16[768,6144]{0,1:T(8,128)(2,1)} async-done(((bf16[768,192]{0,1:T(8,128)(2,1)}), bf16[768,6144]{0,1:T(8,128)(2,1)}) %all-gather.14.cloned.1.call-update) | async-done | bytes 9437200 | tf_op jit(solution)/shard_map/all_gather | solution.py:64
  459.6 6.4 %convolution_convert_fusion.2 = bf16[192,768]{1,0:T(8,128)(2,1)} fusion(bf16[6144,192]{0,1:T(8,128)(2,1)S(1)} %bitcast.20, bf16[768,6144]{0,1:T(8,128)(2,1)} %all-gather.14.cloned.1.call-done), kind=kOutput, calls=%fused_computation.3 | convolution fusion | flops 1812086784 | bytes 12091392 | tf_op jit(solution)/shard_map/dot_general | solution.py:63
  (2 shorter events, 0.0 us)
Async XLA Ops:
  6.5 109.5 %all-gather.6.cloned.1.call-start = ((), (), s32[]{:S(2)}) async-start(), calls=%async_computation.3 | async-start | bytes 9732096 | tf_op jit(solution)/shard_map/all_gather | solution.py:38
  7.3 137.1 %all-gather.10.cloned.1.call-start = ((), (), s32[]{:S(2)}) async-start(), calls=%async_computation.5 | async-start | bytes 2654208 | tf_op jit(solution)/shard_map/all_gather | solution.py:44
  8.0 241.5 %all-gather.8.cloned.1.call-start = ((), (), s32[]{:S(2)}) async-start(), calls=%async_computation.4 | async-start | bytes 9732096 | tf_op jit(solution)/shard_map/all_gather | solution.py:47
  116.1 133.4 %copy-start.1 = (f32[768]{0:T(1024)S(1)}, f32[768]{0:T(1024)}, u32[]{:S(2)}) copy-start(f32[768]{0:T(1024)} %param.8) | copy-start | bytes 9220
  116.1 133.4 %copy-start.2 = (f32[192]{0:T(256)S(1)}, f32[192]{0:T(256)}, u32[]{:S(2)}) copy-start(f32[192]{0:T(256)} %param.9) | copy-start | bytes 2308
  122.5 234.5 %copy-start = (bf16[192,768]{1,0:T(8,128)(2,1)S(1)}, bf16[192,768]{1,0:T(8,128)(2,1)}, u32[]{:S(2)}) copy-start(bf16[192,768]{1,0:T(8,128)(2,1)} %param.6) | copy-start | bytes 884740
  122.5 234.5 %all-gather.12.cloned.1.call-start = ((), (), s32[]{:S(2)}) async-start(), calls=%async_computation.6 | async-start | bytes 9732096 | tf_op jit(solution)/shard_map/all_gather | solution.py:52
  256.6 203.0 %all-gather.14.cloned.1.call-start = ((), (), s32[]{:S(2)}) async-start(), calls=%async_computation.7 | async-start | bytes 9732096 | tf_op jit(solution)/shard_map/all_gather | solution.py:64
Sparse Core Ops, SparseCore 0:
  9.9 106.1 all-gather.5
  117.9 26.3 all-gather.9
  146.9 102.5 all-gather.7
  256.7 100.1 all-gather.11
  359.4 100.1 all-gather.13
where the time goes:
time: 473 us
  waiting for transfers between devices  328 us (69%)
  blocking collectives  102 us (22%)
  matrix products  26.8 us (6%)
  between operations  13.2 us (3%)
    all_gather x1, waiting for transfers between devices, body(): lax.all_gather(projected, 'col', axis=1, tiled=True)  105 us
    all_gather x1, waiting for transfers between devices, body(): scaled_strip = lax.all_gather(scaled, 'col', axis=1, tiled=True)  99.8 us
    all_gather x1, waiting for transfers between devices, body(): lax.all_gather(basis_left, 'col', axis=0, tiled=True)  71.9 us
    all_to_all x2, blocking collectives, sent_to_all(): return lax.all_to_all(copies, axis, split_axis=0, concat_axis=0, tiled=True)  67.3 us
    all_to_all x1, blocking collectives, sent_and_summed(): parts = lax.all_to_all(in_blocks(shard, dim, peers), axis, 0, 0, tiled=True)  34.5 us
    all_gather x1, waiting for transfers between devices, body(): lax.all_gather(basis_right, 'col', axis=1, tiled=True)  27.7 us
    all_gather x1, waiting for transfers between devices, body(): right_strip = lax.all_gather(basis_right, 'row', axis=0, tiled=True)  21.8 us
  transfers between devices with their start and end apart: 5, of which 5 were waited for; matrix products, arithmetic and copies ran while one was open for 3% of the time, Pallas kernels for 0%

commit v1 on v0

v1 whole, which is shorter than its diff:
```python
import jax
import jax.numpy as jnp
from jax import lax
from jax.experimental import pallas as pl
from jax.experimental.pallas import tpu as pltpu
from jax.sharding import PartitionSpec as P

MESH = pl.DeviceIdType.MESH
B = 384
H = B // 2
Q = B // 4
R = B // 8
NX, NY, NZ = 4, 4, 8


def kernel(
    ct_ref, qa_ref, qbt_ref, el_ref, er_ref, out_ref,
    cs, qas, qbs, ps, ss, hp, hs, qb2, acc, els, ers, er_col,
    rs_t, rs_a, rs_b, rs_mid, rs_t2, rs_a2, rs_b2, h_own, xo, xin,
    swap_send, swap_recv, z_recv, xy_recv, rs_recv, fin_send, fin_recv,
    z_send, xy_send, rs_send,
):
    r, c = lax.axis_index("row"), lax.axis_index("col")
    y, core, z, x = r // 2, r % 2, c // 4, c % 4
    g1, g2 = z * 2 + core, y * 4 + x

    def dev(dx=0, dy=0, dz=0):
        return {
            "row": ((y + dy + NY) % NY) * 2 + core,
            "col": ((z + dz + NZ) % NZ) * 4 + (x + dx + NX) % NX,
        }

    sibling = {"row": y * 2 + 1 - core, "col": c}

    def remote(src, dst, send, recv, device):
        return pltpu.make_async_remote_copy(
            src_ref=src, dst_ref=dst, send_sem=send, recv_sem=recv,
            device_id=device, device_id_type=MESH,
        )

    def landed(dst, sem):
        pltpu.make_async_copy(dst, dst, sem).wait()

    barrier = pltpu.get_barrier_semaphore()
    greeted = [dev(dy=1), dev(dy=-1), dev(dz=1), dev(dz=-1), sibling]
    for dx in (1, 2, 3):
        for k in (core, 1 - core):
            greeted.append({"row": y * 2 + k, "col": z * 4 + (x + dx) % NX})
    for device in greeted:
        pl.semaphore_signal(barrier, inc=1, device_id=device, device_id_type=MESH)
    pl.semaphore_wait(barrier, len(greeted))

    half_x, odd_x = x // 2, x % 2

    def exchange(pieces, send, recv, act, only=(0, 1, 2, 3, 4), halves=(0, 1)):
        for h in halves:
            to_x = 2 * core + h
            own = jnp.logical_and(to_x == x, half_x == core)
            for n, (src, dst) in enumerate(pieces(h, to_x)):
                if n not in only:
                    continue

                @pl.when(own)
                def _(n=n, src=src, dst=dst):
                    if act == "start":
                        pltpu.make_async_copy(src, dst, recv.at[n, odd_x]).start()

                @pl.when(jnp.logical_not(own))
                def _(n=n, src=src, dst=dst, h=h, to_x=to_x):
                    copy = remote(
                        src, dst, send.at[n, h], recv.at[n, odd_x],
                        {"row": y * 2 + half_x, "col": z * 4 + to_x},
                    )
                    if act == "start":
                        copy.start()
                    else:
                        copy.wait_send()

    def first_pieces(h, to_x):
        lanes = pl.ds(h * B, B)
        rows = pl.ds(pl.multiple_of(odd_x * H, H), H)
        return (
            (qa_ref.at[:, lanes], qas.at[z * 2 + half_x, rows, :]),
            (ct_ref.at[:, lanes], cs.at[y * 4 + to_x, rows, :]),
            (qbt_ref.at[:, lanes], qbs.at[y * 4 + to_x, rows, :]),
            (el_ref.at[:, lanes], els.at[odd_x]),
            (er_ref, ers.at[odd_x]),
        )

    def first_landed(n):
        for s in (0, 1):
            rows = pl.ds(s * H, H)
            dst = (
                qas.at[g1, rows, :], cs.at[g2, rows, :], qbs.at[g2, rows, :], els.at[s], ers.at[s],
            )[n]
            landed(dst, swap_recv.at[n, s])

    def z_gather(buf, bank, fine=False):
        def at(dz, half, k=core):
            zz = (z + dz + NZ) % NZ
            if fine:
                return buf.at[zz, pl.ds(k * 8 + half * 4, 4)]
            return buf.at[zz * 2 + k, pl.ds(half * H, H), :]

        def last(way, half):
            return 4 if (way == 1) == (half == 0) else 3

        def slot(way, half, step):
            return z_recv.at[bank, (0 if way == 1 else 8) + half * 4 + step - 1]

        def push(dz, half, way, step):
            ref = at(dz, half)
            remote(ref, ref, z_send.at[bank], slot(way, half, step), dev(dz=way)).start()

        def across(dz, half):
            ref = at(dz, half)
            remote(ref, ref, z_send.at[bank], z_recv.at[bank, 16 + (dz % NZ) * 2 + half], sibling).start()

        def begin():
            for half in (0, 1):
                push(0, half, 1, 1)
                push(0, 1 - half, -1, 1)
            for half in (0, 1):
                across(0, half)

        def arrive(way, half, step):
            landed(at(-way * step, half), slot(way, half, step))
            if step < last(way, half):
                push(-way * step, half, way, step + 1)
            across(-way * step, half)

        events = []
        for way in (1, -1):
            for half in (0, 1):
                for step in range(1, last(way, half) + 1):
                    first = (way == 1) == (half == 0)
                    when = (2 * step - (1 if first else 0)) * 3.2 + 2.2
                    events.append((when, lambda w=way, h=half, s=step: arrive(w, h, s)))

        def crossed(dz):
            for half in (0, 1):
                landed(at(dz, half, 1 - core), z_recv.at[bank, 16 + dz % NZ * 2 + half])

        def sent():
            landed(cs.at[pl.ds(0, 15)], z_send.at[bank])

        def finish():
            for dz in range(NZ):
                crossed(dz)
            sent()

        return begin, events, finish, crossed, sent

    def xy_gather(buf, bank):
        events, begins = [], [[], []]
        for part in (0, 1):
            base = part * H

            def at(i, j, lo=0, n=H, part=part, base=base):
                dy, dx = (j, i) if part == 0 else (i, j)
                return buf.at[((y + dy + NY) % NY) * 4 + (x + dx + NX) % NX, pl.ds(base + lo, n), :]

            def slot(kind, i, way, hop, part=part):
                return xy_recv.at[bank, part * 20 + (kind + (i % 4 if kind else 0)) * 4 + (0 if way == 1 else 2) + hop - 1]

            def along(axis, way, part=part):
                return dev(dx=way) if (axis == 0) == (part == 0) else dev(dy=way)

            def push(ref, axis, way, sem, along=along):
                remote(ref, ref, xy_send.at[bank], sem, along(axis, way)).start()

            def second(i, at=at, slot=slot, push=push):
                for way in (1, -1):
                    push(at(i, 0), 1, way, slot(1, i, way, 1))

            def first_start(at=at, slot=slot, push=push):
                for way in (1, -1):
                    push(at(0, 0), 0, way, slot(0, 0, way, 1))

            begins[0].append(first_start)
            begins[1].append(lambda second=second: second(0))

            def first_hop(way, at=at, slot=slot, push=push, second=second):
                landed(at(-way, 0), slot(0, 0, way, 1))
                push(at(-way, 0, 0 if way == 1 else Q, Q), 0, way, slot(0, 0, way, 2))

            def first_far(at=at, slot=slot, second=second):
                for way in (1, -1):
                    landed(at(2, 0, 0 if way == 1 else Q, Q), slot(0, 0, way, 2))
                second(2)

            def second_hop(i, way, at=at, slot=slot, push=push):
                landed(at(i, -way), slot(1, i, way, 1))
                push(at(i, -way, 0 if way == 1 else Q, Q), 1, way, slot(1, i, way, 2))

            def second_far(i, way, at=at, slot=slot):
                landed(at(i, 2, 0 if way == 1 else Q, Q), slot(1, i, way, 2))

            for way in (1, -1):
                events.append((5.60, lambda f=first_hop, w=way: f(w)))
                events.append((5.61 if way == 1 else 5.62, lambda f=second, w=way: f(-w)))
                events.append((8.7, lambda f=second_hop, w=way: f(0, w)))
                events.append((13.4, lambda f=second_hop, w=way: f(-1, w)))
                events.append((16.5, lambda f=second_hop, w=way: f(1, w)))
                events.append((21.2, lambda f=second_hop, w=way: f(2, w)))
                for when, i in ((18.3, 0), (22.8, -1), (24.3, 1), (25.9, 2)):
                    events.append((when, lambda f=second_far, i=i, w=way: f(i, w)))
            events.append((10.4, first_far))

        def begin():
            for stage in begins:
                for start in stage:
                    start()

        def finish():
            landed(buf.at[pl.ds(0, 15)], xy_send.at[bank])

        return begin, events, finish

    def xy_sum(ready):
        events = []
        for n, dz in enumerate((0, -1, 1, -2, 2, -3, 3, 4)):
            part, way = n % 2, 1 if n // 2 % 2 == 0 else -1
            zc = (z + dz + NZ) % NZ
            me = y if part == 0 else x

            def slab(i, part=part, zc=zc):
                if part == 0:
                    return hp.at[zc, :, (x + i + NX) % NX]
                return hp.at[zc, (y + i + NY) % NY]

            def push(src, dst, what, axis, to, part=part, n=n):
                device = dev(dx=to) if (axis == 0) == (part == 0) else dev(dy=to)
                remote(src, dst, rs_send, rs_recv.at[n, what], device).start()

            def begin(dz=dz, zc=zc, n=n, way=way, slab=slab, push=push):
                ready(dz)

                @pl.loop(0, 2)
                def _(k):
                    part = lax.dot_general(
                        ss[2 * zc + k], qas[g1], (((1,), (1,)), ((), ())), preferred_element_type=jnp.float32
                    )
                    hp[zc, pl.ds(2 * k, 2)] = part.astype(jnp.bfloat16).reshape(2, 4, R, B)

                push(slab(2), rs_t.at[n], 0, 0, way)
                push(slab(-way), rs_b.at[n], 1, 0, -way)

            def relay(n=n, way=way, slab=slab, push=push):
                landed(rs_t.at[n], rs_recv.at[n, 0])
                ref = slab(way)
                for j in range(4):
                    ref[j] = (ref[j].astype(jnp.float32) + rs_t[n, j].astype(jnp.float32)).astype(jnp.bfloat16)
                push(ref, rs_a.at[n], 2, 0, way)

            def middle(n=n, way=way, slab=slab, push=push, me=me):
                landed(rs_b.at[n], rs_recv.at[n, 1])
                landed(rs_a.at[n], rs_recv.at[n, 2])
                ref = slab(0)
                for j in range(4):
                    total = ref[j].astype(jnp.float32) + rs_a[n, j].astype(jnp.float32) + rs_b[n, j].astype(jnp.float32)
                    rs_mid[n, j] = total.astype(jnp.bfloat16)
                push(rs_mid.at[n, (me + 2) % 4], rs_t2.at[n], 3, 1, way)
                push(rs_mid.at[n, (me - way + 4) % 4], rs_b2.at[n], 4, 1, -way)

            def relay2(n=n, way=way, push=push, me=me):
                landed(rs_t2.at[n], rs_recv.at[n, 3])
                ref = rs_mid.at[n, (me + way + 4) % 4]
                ref[...] = (ref[...].astype(jnp.float32) + rs_t2[n].astype(jnp.float32)).astype(jnp.bfloat16)
                push(ref, rs_a2.at[n], 5, 1, way)

            def last(n=n, me=me, zc=zc):
                landed(rs_b2.at[n], rs_recv.at[n, 4])
                landed(rs_a2.at[n], rs_recv.at[n, 5])
                total = rs_mid[n, me].astype(jnp.float32) + rs_a2[n].astype(jnp.float32) + rs_b2[n].astype(jnp.float32)
                h_own[zc] = total.astype(jnp.bfloat16)

            when = (1.5, 9.9, 10.0, 16.3, 16.4, 22.7, 22.8, 25.9)[n]
            for later, event in zip((0.0, 6.4, 12.6, 16.2), (begin, relay, middle, relay2)):
                events.append((when + later, event))
            events.append((44.0 + 0.1 * n, last))
        return events

    def run(*plans):
        for _, event in sorted((e for plan in plans for e in plan), key=lambda e: e[0]):
            event()

    def product(a, b, rows=slice(None)):
        def four(k):
            wide = jnp.concatenate([a[k + n, rows, :] for n in range(4)], axis=1)
            return jnp.dot(wide, b(k), preferred_element_type=jnp.float32)

        acc[rows, :] = four(0)

        @pl.loop(1, 4)
        def _(k):
            acc[rows, :] += four(4 * k)

    exchange(first_pieces, swap_send, swap_recv, "start", (0, 1))
    qa_plan, c_plan = z_gather(qas, 0), xy_gather(cs, 0)
    first_landed(0)
    qa_plan[0]()
    first_landed(1)
    c_plan[0]()
    late = lambda: exchange(first_pieces, swap_send, swap_recv, "start", (2, 3, 4))
    run(qa_plan[1], c_plan[1], [(18.1, late)])
    qa_plan[2]()
    c_plan[2]()

    def rows_of(ref):
        return lambda k: ref[pl.ds(k, 4)].reshape(4 * B, B)

    product(cs, rows_of(qas))
    ps[g1] = acc[...].astype(jnp.bfloat16)
    p_plan, qb_plan = z_gather(ps, 1), xy_gather(qbs, 1)
    p_plan[0]()
    first_landed(2)
    qb_plan[0]()
    first_landed(3)
    first_landed(4)
    diagonal = lax.broadcasted_iota(jnp.int32, (H, H), 0) == lax.broadcasted_iota(jnp.int32, (H, H), 1)
    for s in (0, 1):
        column = jnp.sum(jnp.where(diagonal, ers[s], 0.0), axis=1, keepdims=True)
        er_col[pl.ds(s * H, H), :] = jnp.broadcast_to(column, (H, 128))
    qb2[z, pl.ds(core * 8, 8)] = qbs[g2].reshape(8, R, B)
    run(p_plan[1], qb_plan[1])
    exchange(first_pieces, swap_send, swap_recv, "wait")
    p_plan[2]()
    qb_plan[2]()

    product(qbs, rows_of(ps))
    ss[g1] = (acc[...] / (els[0] + er_col[:, 0:1])).astype(jnp.bfloat16)
    s_plan, qb2_plan = z_gather(ss, 0), z_gather(qb2, 1, fine=True)
    s_plan[0]()
    start, cut = 25.0, 39.0
    early = [(t + start, e) for t, e in qb2_plan[1] if t + start <= cut]
    after = [(t + start - cut, e) for t, e in qb2_plan[1] if t + start > cut]
    run(s_plan[1], xy_sum(s_plan[3]), [(start, qb2_plan[0])], early)
    hs[g2] = h_own[...].reshape(B, B).astype(jnp.float32).T.astype(jnp.bfloat16)
    h_plan = xy_gather(hs, 0)
    h_plan[0]()
    s_plan[4]()
    landed(cs.at[pl.ds(0, 15)], rs_send)
    run(h_plan[1], after)
    qb2_plan[2]()
    h_plan[2]()

    def rows_across(k):
        return jnp.concatenate([qb2[:, k + n].reshape(B, B) for n in range(4)], axis=0)

    def last_pieces(h, to_x):
        return ((xo.at[pl.ds(h * H, H), :], xin.at[odd_x]),)

    for h in (0, 1):
        rows = pl.ds(h * H, H)
        product(hs, rows_across, rows)
        xo[rows, :] = acc[rows, :].astype(jnp.bfloat16)
        exchange(last_pieces, fin_send, fin_recv, "start", halves=(h,))
    for s in (0, 1):
        landed(xin.at[s], fin_recv.at[0, s])
        out_ref[:, pl.ds(s * B, B)] = xin[s]
    exchange(last_pieces, fin_send, fin_recv, "wait")


def body(rhs, basis_left, basis_right, eig_left, eig_right):
    strip = pltpu.VMEM((16, B, B), jnp.bfloat16)
    slabs, pieces = pltpu.VMEM((8, 4, R, B), jnp.bfloat16), pltpu.VMEM((8, R, B), jnp.bfloat16)
    dma = pltpu.SemaphoreType.DMA
    return pl.pallas_call(
        kernel,
        out_shape=jax.ShapeDtypeStruct((H, 2 * B), jnp.bfloat16),
        in_specs=[pl.BlockSpec(memory_space=pltpu.VMEM)] * 5,
        out_specs=pl.BlockSpec(memory_space=pltpu.VMEM),
        scratch_shapes=[
            strip, strip, strip, strip, strip,
            pltpu.VMEM((8, 4, 4, R, B), jnp.bfloat16),
            strip,
            pltpu.VMEM((8, 16, R, B), jnp.bfloat16),
            pltpu.VMEM((B, B), jnp.float32),
            pltpu.VMEM((2, 1, B), jnp.float32),
            pltpu.VMEM((2, 1, H), jnp.float32),
            pltpu.VMEM((B, 128), jnp.float32),
            slabs, slabs, slabs, slabs, pieces, pieces, pieces, pieces,
            pltpu.VMEM((B, B), jnp.bfloat16),
            pltpu.VMEM((2, H, B), jnp.bfloat16),
            dma((5, 2)), dma((5, 2)), dma((2, 32)), dma((2, 40)), dma((8, 6)), dma((1, 2)), dma((1, 2)),
            dma((2,)), dma((2,)), dma,
        ],
        compiler_params=pltpu.CompilerParams(
            collective_id=0, has_side_effects=True, vmem_limit_bytes=60 * 1024 * 1024
        ),
    )(
        rhs.T,
        basis_left,
        basis_right.T,
        eig_left[None, :],
        eig_right[None, :],
    )


def solution(mesh):
    in_specs = (P("row", "col"), P("col", "row"), P("row", "col"), P("row"), P("col"))
    out_specs = P("col", "row")
    return jax.shard_map(body, mesh=mesh, in_specs=in_specs, out_specs=out_specs, check_vma=False)
```

time: 473 us -> 168 us (0.36)
  waiting for transfers between devices: 328 us -> 0 us
  Pallas kernels: 0 us -> 165 us
  blocking collectives: 102 us -> 0 us
  matrix products: 26.8 us -> 0 us
  between operations: 13.2 us -> 0.01 us
    all_gather x5 -> x0, waiting for transfers between devices: 326 us -> none  [the longest x1 105 us: body(): lax.all_gather(projected, 'col', axis=1, tiled=True)]
    pallas_call x0 -> x1, Pallas kernels: none -> 165 us  [body(): pl.pallas_call(kernel, out_shape=jax.ShapeDtypeStruct((H, 2 * B), jnp.bfl...]
    all_to_all x3 -> x0, blocking collectives: 102 us -> none  [the longest x2 67.3 us: sent_to_all(): return lax.all_to_all(copies, axis, split_axis=0, concat_axis=0, tiled=True)]
    dot_general x4 -> x0, matrix products: 26.8 us -> none  [the longest x1 7.11 us: body(): jnp.dot(lax.all_gather(projected, 'col', axis=1, tiled=True), chosen, pre...]
  transfers between devices with their start and end apart: 5 -> 0, of which waited for: 5 -> 0; matrix products, arithmetic and copies ran while one was open for 3% -> 0% of each run, Pallas kernels for 0% -> 0%
where the time goes in v1:
time: 168 us
  Pallas kernels  165 us (98%)
  local copies, waits for them, and re-layouts  2.96 us (2%)
    pallas_call x1, Pallas kernels, body(): pl.pallas_call(kernel, out_shape=jax.ShapeDtypeStruct((H, 2 * B), jnp.bfl...  165 us

profile of v1, /device:TPU:1, one launch (start us, length us, event | category | flops | bytes accessed | tf_op | source)
XLA Modules:
  0.0 168.1 jit_solution(4289237595608268886)
XLA Ops:
  0.0 0.0 copy-start
  0.0 0.7 copy-done
  0.7 0.6 broadcast_in_dim.6.el_ref
  1.3 165.1 %shard_map.55 = bf16[192,768]{1,0:T(8,128)(2,1)} custom-call(bf16[192,768]{1,0:T(8,128)(2,1)} %bitcast.3, bf16[192,768]{1,0:T(8,128)(2,1)} %qa_ref.1, bf16[192,768]{1,0:T(8,128)(2,1)} %bitcast.4, f32[1,768]{1,0:T(1,128)} %broadcast_in_dim.6.el_ref, f32[1,192]{1,0:T(1,128)} %bitcast.5), custom_call_target="tpu_custom_call" | custom-call | tf_op jit(solution)/shard_map/pallas_call | solution.py:369
  166.4 1.7 %copy.7 = bf16[192,768]{1,0:T(8,128)(2,1)} copy(bf16[192,768]{1,0:T(8,128)(2,1)} %shard_map.55) | data formatting | bytes 589824
Async XLA Ops:
  0.0 0.7 copy-start

commit v2 on v1

--- a/solution.py
+++ b/solution.py
@@ -11,14 +11,35 @@
 Q = B // 4
 R = B // 8
 NX, NY, NZ = 4, 4, 8
+ROUTES = ((1, 1, 1, 1), (1, 1, 0, 1), (0, -1, 1, -1), (1, -1, 0, -1), (0, 1, 1, 1), (1, 1, 0, 1), (0, -1, 1, -1), (1, 1, 0, -1))
+ORDER = (0, -1, 1, -2, 2, -3, 3, 4)
+
+WAITS = (
+    (
+        0, 10, 14, 24, 35, 45, 15, 36, 25, 46, 4, 7, 16, 26, 37, 47, 1, 11, 34, 55, 5, 8, 17, 27, 38, 48, 2, 12, 18,
+        28, 39, 49, 6, 9, 19, 29, 40, 50, 56, 3, 13, 20, 30, 41, 51, 21, 31, 42, 52, 22, 32, 43, 53, 23, 33, 44, 54,
+    ),
+    (
+        0, 10, 14, 24, 35, 45, 15, 36, 25, 46, 4, 7, 16, 26, 37, 47, 34, 55, 1, 11, 17, 27, 38, 48, 5, 8, 18, 28,
+        39, 49, 2, 12, 19, 29, 40, 50, 6, 9, 3, 13, 20, 30, 41, 51, 21, 31, 42, 52, 22, 32, 43, 53, 23, 33, 44, 54,
+    ),
+    (
+        14, 0, 10, 15, 4, 7, 26, 38, 1, 11, 16, 5, 8, 27, 50, 39, 62, 17, 2, 12, 6, 9, 110, 28, 51, 40, 74, 63, 86,
+        18, 3, 13, 29, 98, 52, 111, 121, 41, 64, 75, 87, 115, 118, 53, 19, 21, 99, 30, 65, 112, 122, 88, 22, 54, 23,
+        42, 76, 116, 119, 20, 31, 89, 55, 57, 45, 113, 123, 100, 77, 33, 56, 24, 66, 32, 90, 58, 117, 120, 101, 59,
+        78, 43, 34, 60, 93, 69, 35, 114, 124, 102, 125, 126, 46, 79, 127, 128, 47, 129, 130, 67, 131, 132, 36, 133,
+        25, 44, 91, 103, 61, 81, 80, 105, 70, 71, 48, 92, 94, 82, 106, 95, 83, 107, 104, 68, 49, 37, 96, 72, 108,
+        84, 97, 73, 109, 85,
+    ),
+)
 
 
 def kernel(
     ct_ref, qa_ref, qbt_ref, el_ref, er_ref, out_ref,
     cs, qas, qbs, ps, ss, hp, hs, qb2, acc, els, ers, er_col,
-    rs_t, rs_a, rs_b, rs_mid, rs_t2, rs_a2, rs_b2, h_own, xo, xin,
-    swap_send, swap_recv, z_recv, xy_recv, rs_recv, fin_send, fin_recv,
-    z_send, xy_send, rs_send,
+    rs_t, rs_a, rs_b, rs_mid, rs_t2, rs_a2, rs_b2, xo, xin,
+    swap_send, swap_recv, z_recv, xy_recv, rs_recv, ag_recv, fin_send, fin_recv,
+    z_send, xy_send, rs_send, ag_send,
 ):
     r, c = lax.axis_index("row"), lax.axis_index("col")
     y, core, z, x = r // 2, r % 2, c // 4, c % 4
@@ -52,8 +73,8 @@
 
     half_x, odd_x = x // 2, x % 2
 
-    def exchange(pieces, send, recv, act, only=(0, 1, 2, 3, 4), halves=(0, 1)):
-        for h in halves:
+    def exchange(pieces, send, recv, act, only=(0, 1, 2, 3, 4)):
+        for h in (0, 1):
             to_x = 2 * core + h
             own = jnp.logical_and(to_x == x, half_x == core)
             for n, (src, dst) in enumerate(pieces(h, to_x)):
@@ -83,7 +104,7 @@
             (qa_ref.at[:, lanes], qas.at[z * 2 + half_x, rows, :]),
             (ct_ref.at[:, lanes], cs.at[y * 4 + to_x, rows, :]),
             (qbt_ref.at[:, lanes], qbs.at[y * 4 + to_x, rows, :]),
-            (el_ref.at[:, lanes], els.at[odd_x]),
+            (el_ref, els.at[odd_x]),
             (er_ref, ers.at[odd_x]),
         )
 
@@ -219,8 +240,8 @@
 
     def xy_sum(ready):
         events = []
-        for n, dz in enumerate((0, -1, 1, -2, 2, -3, 3, 4)):
-            part, way = n % 2, 1 if n // 2 % 2 == 0 else -1
+        for n, dz in enumerate(ORDER):
+            part, way, apart, away = ROUTES[n]
             zc = (z + dz + NZ) % NZ
             me = y if part == 0 else x
 
@@ -273,28 +294,77 @@
                 landed(rs_b2.at[n], rs_recv.at[n, 4])
                 landed(rs_a2.at[n], rs_recv.at[n, 5])
                 total = rs_mid[n, me].astype(jnp.float32) + rs_a2[n].astype(jnp.float32) + rs_b2[n].astype(jnp.float32)
-                h_own[zc] = total.astype(jnp.bfloat16)
+                hs[g2, n] = total.astype(jnp.bfloat16)
+
+            def at(i, j, part=apart, n=n):
+                dy, dx = (j, i) if part == 0 else (i, j)
+                return hs.at[((y + dy + NY) % NY) * 4 + (x + dx + NX) % NX, n]
+
+            def share(ref, what, axis, to, part=apart, n=n):
+                device = dev(dx=to) if (axis == 0) == (part == 0) else dev(dy=to)
+                remote(ref, ref, ag_send, ag_recv.at[n, what], device).start()
+
+            def second(i, n=n, way=away, at=at, share=share):
+                share(at(i, 0), 3 + 3 * (i % 4), 1, way)
+                share(at(i, 0), 4 + 3 * (i % 4), 1, -way)
+
+            def share0(n=n, way=away, at=at, share=share, last=last, second=second):
+                last()
+                share(at(0, 0), 0, 0, way)
+                share(at(0, 0), 1, 0, -way)
+                second(0)
+
+            def share1(n=n, way=away, at=at, share=share, second=second):
+                landed(at(-way, 0), ag_recv.at[n, 0])
+                share(at(-way, 0), 2, 0, way)
+                second(-way)
+                landed(at(way, 0), ag_recv.at[n, 1])
+                second(way)
+
+            def relay3(i, n=n, way=away, at=at, share=share):
+                landed(at(i, -way), ag_recv.at[n, 3 + 3 * (i % 4)])
+                share(at(i, -way), 5 + 3 * (i % 4), 1, way)
+
+            def share2(n=n, at=at, second=second):
+                landed(at(2, 0), ag_recv.at[n, 2])
+                second(2)
+
+            def rest(n=n, way=away, at=at, zc=zc):
+                for i in range(4):
+                    landed(at(i, way), ag_recv.at[n, 4 + 3 * i])
+                    landed(at(i, 2), ag_recv.at[n, 5 + 3 * i])
+                wide = jnp.concatenate([ps[2 * zc], ps[2 * zc + 1]], axis=1)
+                acc[...] += lax.dot_general(
+                    wide, hs[:, n].reshape(2 * B, B), (((1,), (0,)), ((), ())), preferred_element_type=jnp.float32
+                )
 
             when = (1.5, 9.9, 10.0, 16.3, 16.4, 22.7, 22.8, 25.9)[n]
             for later, event in zip((0.0, 6.4, 12.6, 16.2), (begin, relay, middle, relay2)):
                 events.append((when + later, event))
-            events.append((44.0 + 0.1 * n, last))
+            when = (34.0, 36.0, 36.1, 40.0, 40.1, 44.5, 44.6, 46.5)[n]
+            for later, event in zip((0.0, 4.4, 8.8), (share0, share1, share2)):
+                events.append((when + later, event))
+            for later, i in ((4.6, 0), (9.0, -away), (9.1, away), (13.2, 2)):
+                events.append((when + later, lambda f=relay3, i=i: f(i)))
+            events.append((70.0 + 0.1 * n, rest))
         return events
 
-    def run(*plans):
-        for _, event in sorted((e for plan in plans for e in plan), key=lambda e: e[0]):
-            event()
-
-    def product(a, b, rows=slice(None)):
+    def run(order, *plans):
+        events = [event for plan in plans for _, event in plan]
+        assert sorted(order) == list(range(len(events)))
+        for n in order:
+            events[n]()
+
+    def product(a, b):
         def four(k):
-            wide = jnp.concatenate([a[k + n, rows, :] for n in range(4)], axis=1)
+            wide = jnp.concatenate([a[k + n] for n in range(4)], axis=1)
             return jnp.dot(wide, b(k), preferred_element_type=jnp.float32)
 
-        acc[rows, :] = four(0)
+        acc[...] = four(0)
 
         @pl.loop(1, 4)
         def _(k):
-            acc[rows, :] += four(4 * k)
+            acc[...] += four(4 * k)
 
     exchange(first_pieces, swap_send, swap_recv, "start", (0, 1))
     qa_plan, c_plan = z_gather(qas, 0), xy_gather(cs, 0)
@@ -303,7 +373,7 @@
     first_landed(1)
     c_plan[0]()
     late = lambda: exchange(first_pieces, swap_send, swap_recv, "start", (2, 3, 4))
-    run(qa_plan[1], c_plan[1], [(18.1, late)])
+    run(WAITS[0], qa_plan[1], c_plan[1], [(21.25, late)])
     qa_plan[2]()
     c_plan[2]()
 
@@ -323,43 +393,50 @@
         column = jnp.sum(jnp.where(diagonal, ers[s], 0.0), axis=1, keepdims=True)
         er_col[pl.ds(s * H, H), :] = jnp.broadcast_to(column, (H, 128))
     qb2[z, pl.ds(core * 8, 8)] = qbs[g2].reshape(8, R, B)
-    run(p_plan[1], qb_plan[1])
+    run(WAITS[1], p_plan[1], qb_plan[1])
     exchange(first_pieces, swap_send, swap_recv, "wait")
     p_plan[2]()
     qb_plan[2]()
 
     product(qbs, rows_of(ps))
-    ss[g1] = (acc[...] / (els[0] + er_col[:, 0:1])).astype(jnp.bfloat16)
+    el_row = jnp.concatenate([els[0, pl.ds(3 * odd_x + n, 1), :] for n in range(3)], axis=1)
+    ss[g1] = (acc[...] / (el_row + er_col[:, 0:1])).astype(jnp.bfloat16)
     s_plan, qb2_plan = z_gather(ss, 0), z_gather(qb2, 1, fine=True)
     s_plan[0]()
-    start, cut = 25.0, 39.0
-    early = [(t + start, e) for t, e in qb2_plan[1] if t + start <= cut]
-    after = [(t + start - cut, e) for t, e in qb2_plan[1] if t + start > cut]
-    run(s_plan[1], xy_sum(s_plan[3]), [(start, qb2_plan[0])], early)
-    hs[g2] = h_own[...].reshape(B, B).astype(jnp.float32).T.astype(jnp.bfloat16)
-    h_plan = xy_gather(hs, 0)
-    h_plan[0]()
+    start = 21.5
+    tail = [(start, qb2_plan[0])] + [(t + start, e) for t, e in qb2_plan[1]] + [(51.5, qb2_plan[2])]
+
+    def turn(dz):
+        zc = (z + dz + NZ) % NZ
+        for k in (0, 1):
+            block = qb2[zc, pl.ds(8 * k, 8)].reshape(B, B)
+            ps[2 * zc + k] = block.astype(jnp.float32).T.astype(jnp.bfloat16)
+
+    tail += [(51.6 + 0.9 * k, lambda dz=dz: turn(dz)) for k, dz in enumerate(ORDER)]
+    acc[...] = jnp.zeros_like(acc)
+    run(WAITS[2], s_plan[1], xy_sum(s_plan[3]), tail)
     s_plan[4]()
     landed(cs.at[pl.ds(0, 15)], rs_send)
-    run(h_plan[1], after)
-    qb2_plan[2]()
-    h_plan[2]()
-
-    def rows_across(k):
-        return jnp.concatenate([qb2[:, k + n].reshape(B, B) for n in range(4)], axis=0)
-
-    def last_pieces(h, to_x):
-        return ((xo.at[pl.ds(h * H, H), :], xin.at[odd_x]),)
-
-    for h in (0, 1):
-        rows = pl.ds(h * H, H)
-        product(hs, rows_across, rows)
-        xo[rows, :] = acc[rows, :].astype(jnp.bfloat16)
-        exchange(last_pieces, fin_send, fin_recv, "start", halves=(h,))
-    for s in (0, 1):
-        landed(xin.at[s], fin_recv.at[0, s])
-        out_ref[:, pl.ds(s * B, B)] = xin[s]
-    exchange(last_pieces, fin_send, fin_recv, "wait")
+    landed(cs.at[pl.ds(0, 15)], ag_send)
+
+    for third in range(3):
+        lanes = pl.ds(third * 128, 128)
+        xo[:, lanes] = acc[lanes, :].T.astype(jnp.bfloat16)
+
+        def last_pieces(h, to_x, lanes=lanes):
+            return tuple((xo.at[pl.ds(h * H, H), lanes], xin.at[odd_x, :, lanes]) for _ in range(3))
+
+        exchange(last_pieces, fin_send, fin_recv, "start", (third,))
+
+    def all_pieces(h, to_x):
+        cuts = [pl.ds(third * 128, 128) for third in range(3)]
+        return tuple((xo.at[pl.ds(h * H, H), lanes], xin.at[odd_x, :, lanes]) for lanes in cuts)
+
+    for third in range(3):
+        for s in (0, 1):
+            landed(xin.at[s, :, pl.ds(third * 128, 128)], fin_recv.at[third, s])
+            out_ref[:, pl.ds(s * B + third * 128, 128)] = xin[s, :, pl.ds(third * 128, 128)]
+    exchange(all_pieces, fin_send, fin_recv, "wait")
 
 
 def body(rhs, basis_left, basis_right, eig_left, eig_right):
@@ -374,17 +451,17 @@
         scratch_shapes=[
             strip, strip, strip, strip, strip,
             pltpu.VMEM((8, 4, 4, R, B), jnp.bfloat16),
-            strip,
+            pltpu.VMEM((16, 8, R, B), jnp.bfloat16),
             pltpu.VMEM((8, 16, R, B), jnp.bfloat16),
             pltpu.VMEM((B, B), jnp.float32),
-            pltpu.VMEM((2, 1, B), jnp.float32),
+            pltpu.VMEM((2, 6, 128), jnp.float32),
             pltpu.VMEM((2, 1, H), jnp.float32),
             pltpu.VMEM((B, 128), jnp.float32),
-            slabs, slabs, slabs, slabs, pieces, pieces, pieces, pieces,
+            slabs, slabs, slabs, slabs, pieces, pieces, pieces,
             pltpu.VMEM((B, B), jnp.bfloat16),
             pltpu.VMEM((2, H, B), jnp.bfloat16),
-            dma((5, 2)), dma((5, 2)), dma((2, 32)), dma((2, 40)), dma((8, 6)), dma((1, 2)), dma((1, 2)),
-            dma((2,)), dma((2,)), dma,
+            dma((5, 2)), dma((5, 2)), dma((2, 32)), dma((2, 40)), dma((8, 6)), dma((8, 15)), dma((3, 2)), dma((3, 2)),
+            dma((2,)), dma((2,)), dma, dma,
         ],
         compiler_params=pltpu.CompilerParams(
             collective_id=0, has_side_effects=True, vmem_limit_bytes=60 * 1024 * 1024
@@ -393,7 +470,7 @@
         rhs.T,
         basis_left,
         basis_right.T,
-        eig_left[None, :],
+        eig_left.reshape(6, 128),
         eig_right[None, :],
     )
 

time: 168 us -> 158 us (0.940)
  Pallas kernels: 165 us -> 156 us
    pallas_call x1, Pallas kernels: 165 us -> 156 us  [body(): pl.pallas_call(kernel, out_shape=jax.ShapeDtypeStruct((H, 2 * B), jnp.bfl...]
where the time goes in v2:
time: 158 us
  Pallas kernels  156 us (99%)
  local copies, waits for them, and re-layouts  1.69 us (1%)
    pallas_call x1, Pallas kernels, body(): pl.pallas_call(kernel, out_shape=jax.ShapeDtypeStruct((H, 2 * B), jnp.bfl...  156 us

profile of v2, /device:TPU:1, one launch (start us, length us, event | category | flops | bytes accessed | tf_op | source)
XLA Modules:
  0.0 158.1 jit_solution(10659970254198900612)
XLA Ops:
  0.0 156.4 %shard_map.55 = bf16[192,768]{1,0:T(8,128)(2,1)} custom-call(bf16[192,768]{1,0:T(8,128)(2,1)} %bitcast.4, bf16[192,768]{1,0:T(8,128)(2,1)} %qa_ref.1, bf16[192,768]{1,0:T(8,128)(2,1)} %bitcast.5, f32[6,128]{1,0:T(8,128)} %bitcast.6, f32[1,192]{1,0:T(1,128)} %bitcast.7), custom_call_target="tpu_custom_call" | custom-call | tf_op jit(solution)/shard_map/pallas_call | solution.py:446
  156.4 1.7 %copy.7 = bf16[192,768]{1,0:T(8,128)(2,1)} copy(bf16[192,768]{1,0:T(8,128)(2,1)} %shard_map.55) | data formatting | bytes 589824

commit v3 on v2

--- a/solution.py
+++ b/solution.py
@@ -35,11 +35,12 @@
 
 
 def kernel(
-    ct_ref, qa_ref, qbt_ref, el_ref, er_ref, out_ref,
+    ct_in, qa_in, qbt_in, el_ref, er_ref, out_ref,
+    ct_ref, qa_ref, qbt_ref,
     cs, qas, qbs, ps, ss, hp, hs, qb2, acc, els, ers, er_col,
     rs_t, rs_a, rs_b, rs_mid, rs_t2, rs_a2, rs_b2, xo, xin,
     swap_send, swap_recv, z_recv, xy_recv, rs_recv, ag_recv, fin_send, fin_recv,
-    z_send, xy_send, rs_send, ag_send,
+    z_send, xy_send, rs_send, ag_send, in_sem,
 ):
     r, c = lax.axis_index("row"), lax.axis_index("col")
     y, core, z, x = r // 2, r % 2, c // 4, c % 4
@@ -61,6 +62,13 @@
 
     def landed(dst, sem):
         pltpu.make_async_copy(dst, dst, sem).wait()
+
+    loads = [
+        pltpu.make_async_copy(src, dst, in_sem.at[n])
+        for n, (src, dst) in enumerate(((qa_in, qa_ref), (ct_in, ct_ref), (qbt_in, qbt_ref)))
+    ]
+    for load in loads:
+        load.start()
 
     barrier = pltpu.get_barrier_semaphore()
     greeted = [dev(dy=1), dev(dy=-1), dev(dz=1), dev(dz=-1), sibling]
@@ -366,7 +374,10 @@
         def _(k):
             acc[...] += four(4 * k)
 
-    exchange(first_pieces, swap_send, swap_recv, "start", (0, 1))
+    for n in (0, 1):
+        loads[n].wait()
+        exchange(first_pieces, swap_send, swap_recv, "start", (n,))
+    loads[2].wait()
     qa_plan, c_plan = z_gather(qas, 0), xy_gather(cs, 0)
     first_landed(0)
     qa_plan[0]()
@@ -441,14 +452,16 @@
 
 def body(rhs, basis_left, basis_right, eig_left, eig_right):
     strip = pltpu.VMEM((16, B, B), jnp.bfloat16)
+    block = pltpu.VMEM((H, 2 * B), jnp.bfloat16)
     slabs, pieces = pltpu.VMEM((8, 4, R, B), jnp.bfloat16), pltpu.VMEM((8, R, B), jnp.bfloat16)
     dma = pltpu.SemaphoreType.DMA
     return pl.pallas_call(
         kernel,
         out_shape=jax.ShapeDtypeStruct((H, 2 * B), jnp.bfloat16),
-        in_specs=[pl.BlockSpec(memory_space=pltpu.VMEM)] * 5,
+        in_specs=[pl.BlockSpec(memory_space=pl.ANY)] * 3 + [pl.BlockSpec(memory_space=pltpu.VMEM)] * 2,
         out_specs=pl.BlockSpec(memory_space=pltpu.VMEM),
         scratch_shapes=[
+            block, block, block,
             strip, strip, strip, strip, strip,
             pltpu.VMEM((8, 4, 4, R, B), jnp.bfloat16),
             pltpu.VMEM((16, 8, R, B), jnp.bfloat16),
@@ -461,7 +474,7 @@
             pltpu.VMEM((B, B), jnp.bfloat16),
             pltpu.VMEM((2, H, B), jnp.bfloat16),
             dma((5, 2)), dma((5, 2)), dma((2, 32)), dma((2, 40)), dma((8, 6)), dma((8, 15)), dma((3, 2)), dma((3, 2)),
-            dma((2,)), dma((2,)), dma, dma,
+            dma((2,)), dma((2,)), dma, dma, dma((3,)),
         ],
         compiler_params=pltpu.CompilerParams(
             collective_id=0, has_side_effects=True, vmem_limit_bytes=60 * 1024 * 1024

time: 158 us -> 158 us (level)
  no operation moved by 1% of the time
where the time goes in v3:
time: 158 us
  Pallas kernels  156 us (99%)
  local copies, waits for them, and re-layouts  1.69 us (1%)
    pallas_call x1, Pallas kernels, body(): pl.pallas_call(kernel, out_shape=jax.ShapeDtypeStruct((H, 2 * B), jnp.bfl...  156 us

profile of v3, /device:TPU:1, one launch (start us, length us, event | category | flops | bytes accessed | tf_op | source)
XLA Modules:
  0.0 157.7 jit_solution(13734558631507760226)
XLA Ops:
  0.0 156.0 %shard_map.55 = bf16[192,768]{1,0:T(8,128)(2,1)} custom-call(bf16[192,768]{1,0:T(8,128)(2,1)} %bitcast.4, bf16[192,768]{1,0:T(8,128)(2,1)} %qa_in.1, bf16[192,768]{1,0:T(8,128)(2,1)} %bitcast.5, f32[6,128]{1,0:T(8,128)} %bitcast.6, f32[1,192]{1,0:T(1,128)} %bitcast.7), custom_call_target="tpu_custom_call" | custom-call | tf_op jit(solution)/shard_map/pallas_call | solution.py:458
  156.0 1.7 %copy.7 = bf16[192,768]{1,0:T(8,128)(2,1)} copy(bf16[192,768]{1,0:T(8,128)(2,1)} %shard_map.55) | data formatting | bytes 589824

commit v4 on v3

--- a/solution.py
+++ b/solution.py
@@ -364,15 +364,12 @@
             events[n]()
 
     def product(a, b):
-        def four(k):
-            wide = jnp.concatenate([a[k + n] for n in range(4)], axis=1)
+        def eight(k):
+            wide = jnp.concatenate([a[k + n] for n in range(8)], axis=1)
             return jnp.dot(wide, b(k), preferred_element_type=jnp.float32)
 
-        acc[...] = four(0)
-
-        @pl.loop(1, 4)
-        def _(k):
-            acc[...] += four(4 * k)
+        acc[...] = eight(0)
+        acc[...] += eight(8)
 
     for n in (0, 1):
         loads[n].wait()
@@ -389,7 +386,7 @@
     c_plan[2]()
 
     def rows_of(ref):
-        return lambda k: ref[pl.ds(k, 4)].reshape(4 * B, B)
+        return lambda k: ref[pl.ds(k, 8)].reshape(8 * B, B)
 
     product(cs, rows_of(qas))
     ps[g1] = acc[...].astype(jnp.bfloat16)

time: 158 us -> 157 us (level)
  no operation moved by 1% of the time
where the time goes in v4:
time: 157 us; the launch traced here: 156 us
  Pallas kernels  155 us (99%)
  local copies, waits for them, and re-layouts  1.69 us (1%)
    pallas_call x1, Pallas kernels, body(): pl.pallas_call(kernel, out_shape=jax.ShapeDtypeStruct((H, 2 * B), jnp.bfl...  155 us

profile of v4, /device:TPU:1, one launch (start us, length us, event | category | flops | bytes accessed | tf_op | source)
XLA Modules:
  0.0 156.5 jit_solution(16370504133412784342)
XLA Ops:
  0.0 154.8 %shard_map.55 = bf16[192,768]{1,0:T(8,128)(2,1)} custom-call(bf16[192,768]{1,0:T(8,128)(2,1)} %bitcast.4, bf16[192,768]{1,0:T(8,128)(2,1)} %qa_in.1, bf16[192,768]{1,0:T(8,128)(2,1)} %bitcast.5, f32[6,128]{1,0:T(8,128)} %bitcast.6, f32[1,192]{1,0:T(1,128)} %bitcast.7), custom_call_target="tpu_custom_call" | custom-call | tf_op jit(solution)/shard_map/pallas_call | solution.py:455
  154.8 1.7 %copy.7 = bf16[192,768]{1,0:T(8,128)(2,1)} copy(bf16[192,768]{1,0:T(8,128)(2,1)} %shard_map.55) | data formatting | bytes 589824
